TPU v7x, 32 devices: a whole 2x2x4 slice. The times are simulated.
32 devices in a mesh: orb: 4 (over x, core), gx: 2 (over y), gyz: 4 (over z).
Axes of the slice: x: 2, y: 2, z: 4, core: 2. Of those that a mesh axis runs over, the one named last changes fastest.
Arguments:
- orbitals: float32 [2, 12, 32, 32, 128], P(None, 'orb', 'gx', 'gyz'), parts along dimension 1, may hold values from -12 to 12
- potential: float32 [32, 32, 128], P('gx', 'gyz'), may hold values from -8 to 60
Outputs:
- evolved: float32 [2, 12, 32, 32, 128], P(None, 'orb', 'gx', 'gyz'), parts along dimension 1
- residual: float32 [2, 12, 32, 32, 128], P(None, 'orb', 'gx', 'gyz'), parts along dimension 1
There are 4 independent parts, one for each index of `orb`. A program takes and returns all parts, laid end to end along the dimension named above; an argument that names none is the same for every part. Nothing has to cross between parts.
All inputs are finite; a program needn't handle non-finite values.
Results may differ from a plain program's by a relative error of at most 0.0003.
Values sent between devices are 32-bit elements; how exact they have to be, the bound alone decides.
No kernel may reach another device: no remote copies, remote signals or barrier semaphores. Data moves between devices by JAX's collectives and lax.ppermute only.
A program may use at most 64 MiB of HBM per device.

v0:
```python
import functools
import math

import jax
import jax.numpy as jnp
from jax import lax
from jax.experimental import pallas as pl
from jax.experimental.pallas import tpu as pltpu
from jax.sharding import PartitionSpec as P


ITERS = 4


SPACING = 0.25
HALF_STEP = 0.05
COEFF_NEAR = 4.0 / 3.0
COEFF_FAR = -1.0 / 12.0
COEFF_SELF = -2.5

RATIO = -COEFF_NEAR / COEFF_FAR
K2 = HALF_STEP * -0.5 / SPACING**2 * COEFF_FAR
DIAGONAL = -0.5 / SPACING**2 * 3.0 * COEFF_SELF
MARGIN = 8
PLANES = 32
WORKING_SET = 40 * 2**20


def with_halo(array, sides, width):
    for axis, dim in sides:
        size, length = (lax.axis_size(axis), array.shape[dim])
        up = [(i, (i + 1) % size) for i in range(size - 1)]
        down = [(j, i) for i, j in up]
        last = lax.slice_in_dim(array, length - width, length, axis=dim)
        leading = lax.slice_in_dim(array, 0, width, axis=dim)
        before = lax.ppermute(last, axis, up)
        after = lax.ppermute(leading, axis, down)
        array = jnp.concatenate([before, array, after], axis=dim)
    return array


def laplace_apply(padded, potential):
    extent = (padded.shape[2] - 4, padded.shape[3] - 4, padded.shape[4] - 4)

    def window(shift_x, shift_y, shift_z):
        return padded[
            :,
            :,
            2 + shift_x : 2 + shift_x + extent[0],
            2 + shift_y : 2 + shift_y + extent[1],
            2 + shift_z : 2 + shift_z + extent[2],
        ]

    center = window(0, 0, 0)
    summed = 3.0 * COEFF_SELF * center
    for offset, weight in ((1, COEFF_NEAR), (2, COEFF_FAR)):
        summed = summed + weight * (
            window(offset, 0, 0)
            + window(-offset, 0, 0)
            + window(0, offset, 0)
            + window(0, -offset, 0)
            + window(0, 0, offset)
            + window(0, 0, -offset)
        )
    return -0.5 / SPACING**2 * summed + potential * center


def pad_depth(vector):
    return jnp.pad(vector, ((0, 0), (0, 0), (0, 0), (0, 0), (2, 2)))


def system(vector, applied):
    return jnp.stack([vector[0] - HALF_STEP * applied[1], vector[1] + HALF_STEP * applied[0]])


def precondition(vector, potential):
    diagonal = HALF_STEP * (3.75 / SPACING**2 + potential)
    divisor = 1.0 + diagonal * diagonal
    return jnp.stack(
        [(vector[0] + diagonal * vector[1]) / divisor, (vector[1] - diagonal * vector[0]) / divisor]
    )


def braket(left, right):
    real_part = jnp.sum(left[0] * right[0] + left[1] * right[1], axis=(1, 2, 3))
    imag_part = jnp.sum(left[0] * right[1] - left[1] * right[0], axis=(1, 2, 3))
    return (real_part, imag_part)


def times_complex(first, second):
    return (
        first[0] * second[0] - first[1] * second[1],
        first[0] * second[1] + first[1] * second[0],
    )


def divide_complex(first, second):
    modulus = second[0] * second[0] + second[1] * second[1]
    return (
        (first[0] * second[0] + first[1] * second[1]) / modulus,
        (first[1] * second[0] - first[0] * second[1]) / modulus,
    )


def scale_complex(coeff, vector):
    real_coef = coeff[0][:, None, None, None]
    imag_coef = coeff[1][:, None, None, None]
    return jnp.stack(
        [
            real_coef * vector[0] - imag_coef * vector[1],
            real_coef * vector[1] + imag_coef * vector[0],
        ]
    )


def distributed(orbitals, potential):
    def apply_shallow(vector):
        padded = with_halo(vector, (("gx", 2), ("gyz", 3)), 2)
        return laplace_apply(pad_depth(padded), potential)

    h_orbitals = apply_shallow(orbitals)
    residual = jnp.stack([2.0 * HALF_STEP * h_orbitals[1], -2.0 * HALF_STEP * h_orbitals[0]])
    evolved = orbitals
    shadow = residual
    direction = residual
    rho_now = lax.psum(braket(shadow, residual), ("gx", "gyz"))
    for iteration in range(ITERS):
        dir_hat = precondition(direction, potential)
        image = system(dir_hat, apply_shallow(dir_hat))
        alpha_step = divide_complex(rho_now, lax.psum(braket(shadow, image), ("gx", "gyz")))
        half_step = residual - scale_complex(alpha_step, image)
        half_hat = precondition(half_step, potential)
        second = system(half_hat, apply_shallow(half_hat))
        cross_local = braket(second, half_step)
        norm_local = jnp.sum(second * second, axis=(0, 2, 3, 4))
        shadow_half = braket(shadow, half_step)
        shadow_second = braket(shadow, second)
        summed = lax.psum(
            (
                cross_local[0],
                cross_local[1],
                norm_local,
                shadow_half[0],
                shadow_half[1],
                shadow_second[0],
                shadow_second[1],
            ),
            ("gx", "gyz"),
        )
        cross_real, cross_imag, norm_second = (summed[0], summed[1], summed[2])
        omega_step = (cross_real / norm_second, cross_imag / norm_second)
        evolved = evolved + scale_complex(alpha_step, dir_hat) + scale_complex(omega_step, half_hat)
        residual = half_step - scale_complex(omega_step, second)
        if iteration + 1 < ITERS:
            along_second = times_complex(omega_step, (summed[5], summed[6]))
            rho_next = (summed[3] - along_second[0], summed[4] - along_second[1])
            beta_step = times_complex(
                divide_complex(rho_next, rho_now), divide_complex(alpha_step, omega_step)
            )
            direction = residual + scale_complex(
                beta_step, direction - scale_complex(omega_step, image)
            )
            rho_now = rho_next
    return (evolved, residual)


class Layout:
    def __init__(self, groups, rows, columns, count):
        self.groups, self.rows, self.columns, self.count = groups, rows, columns, count
        self.width = -(-count // rows)
        self.segments = columns // self.width
        self.fits = columns % self.width == 0
        inner = [(da, dc) for da in range(rows) for dc in range(self.width)]
        self.near = [(da, 0, dc) for da, dc in inner]
        self.far = [(da, ds, dc) for ds in range(1, self.segments) for da, dc in inner]
        self.across = [(0, ds, 0) for ds in range(1, self.segments)]

    def here(self):
        b = lax.axis_index("gyz")
        return lax.axis_index("gx"), b // self.width, lax.rem(b, self.width)

    def solved_by(self, place):
        q = self.solves(place)
        return jnp.where(lax.rem(lax.axis_index("orb"), 2) == 0, q, self.rows * self.width - 1 - q)

    def moved(self, place, offset, sign=1):
        sizes = (self.rows, self.segments, self.width)
        return tuple(
            p if o == 0 else lax.rem(p + (o if sign > 0 else n - o), n)
            for p, o, n in zip(place, offset, sizes)
        )

    def solves(self, place):
        row = place[0] + place[1]
        row = row % self.rows if isinstance(row, int) else lax.rem(row, self.rows)
        return row * self.width + place[2]

    def owned(self, group, place):
        q = self.solves(place)
        return q if group % 2 == 0 else self.rows * self.width - 1 - q

    def deliveries(self):
        places = [(a, b) for a in range(self.rows) for b in range(self.columns)]
        classes = {}
        for parity in range(2):
            owner = {p: self.owned(parity, (p[0], p[1] // self.width, p[1] % self.width)) for p in places}
            for target in places:
                for q in range(self.count):
                    if owner[target] == q:
                        continue
                    hops = lambda p: abs(p[0] - target[0]) + abs(p[1] - target[1])
                    source = min((p for p in places if owner[p] == q), key=hops)
                    step = (target[0] != source[0], target[1] - source[1])
                    classes.setdefault(step, []).append((parity, source, target, q))
        rounds = []
        for step in sorted(classes, key=lambda s: (-int(s[0]) - abs(s[1]), s)):
            for r in rounds:
                busy = {(m[0], m[1], 0) for m in r} | {(m[0], m[2], 1) for m in r}
                if not any((m[0], m[1], 0) in busy or (m[0], m[2], 1) in busy for m in classes[step]):
                    r += classes[step]
                    break
            else:
                rounds.append(list(classes[step]))
        return rounds

    def looked_up(self, entries):
        parity = lax.rem(lax.axis_index("orb"), 2)
        index = (parity * self.rows + lax.axis_index("gx")) * self.columns + lax.axis_index("gyz")
        value = jnp.int32(-1)
        for (p, (a, b)), entry in entries.items():
            value = jnp.where(index == (p * self.rows + a) * self.columns + b, entry, value)
        return value

    def pairs(self, offset, to_owner):
        found = []
        for g in range(self.groups):
            for a in range(self.rows):
                for b in range(self.columns):
                    place = (a, b // self.width, b % self.width)
                    sizes = (self.rows, self.segments, self.width)
                    other = tuple((p + o) % n for p, o, n in zip(place, offset, sizes))
                    source, target = (other, place)
                    if not to_owner or self.owned(g, target) < self.count:
                        found.append((self.linear(g, source), self.linear(g, target)))
        return found

    def linear(self, g, place):
        return (g * self.rows + place[0]) * self.columns + place[1] * self.width + place[2]


def complex_mul(first, second):
    return (
        first[0] * second[0] - first[1] * second[1],
        first[0] * second[1] + first[1] * second[0],
    )


def pack_far_kernel(layout, orbitals_ref, *out_refs):
    here = layout.here()
    for offset, out_ref in zip(layout.far, out_refs):
        q = jnp.minimum(layout.solved_by(layout.moved(here, offset, -1)), layout.count - 1)
        out_ref[0] = orbitals_ref[0, q]
        out_ref[1] = orbitals_ref[1, q]


def pack_near_kernel(layout, orbitals_ref, potential_ref, *refs):
    others, out_refs = (refs[: len(layout.across)], refs[len(layout.across) :])
    here = layout.here()
    for offset, out_ref in zip(layout.near[1:], out_refs):
        q = jnp.minimum(layout.solved_by(layout.moved(here, offset, -1)), layout.count - 1)
        out_ref[0] = orbitals_ref[0, q]
        out_ref[1] = orbitals_ref[1, q]
        for slot, ref in enumerate((potential_ref,) + tuple(others)):
            out_ref[2 + slot] = ref[...]


def total(parts):
    return jnp.sum(jnp.sum(parts, axis=0, keepdims=True), axis=1, keepdims=True)


def fold(product):
    return jnp.sum(product.reshape(-1, 8, product.shape[-1]), axis=0)


def solve_kernel(layout, *refs):
    near, far, across = (layout.near, layout.far, layout.across)
    orbitals_ref, potential_ref = refs[:2]
    refs = refs[2:]
    pots, refs = (refs[: len(across)], refs[len(across) :])
    near_refs, refs = (refs[: len(near) - 1], refs[len(near) - 1 :])
    far_refs, refs = (refs[: len(far)], refs[len(far) :])
    rounds = layout.deliveries()
    outs, scratch = (refs[: 1 + len(rounds)], refs[1 + len(rounds) :])
    diag, inv, padded_d, padded_h, evolved, res, shadow, direc, image, second = scratch
    bx, by, nz = potential_ref.shape
    nx, ny = (bx * layout.rows, by * layout.columns)
    planes = math.gcd(nx, PLANES)
    here = layout.here()

    def corner(offset):
        a, s, c = layout.moved(here, offset)
        return a * bx, pl.multiple_of((s * layout.width + c) * by, 8)

    zero_edge = jnp.zeros((2, 2, ny + 2 * MARGIN, nz), jnp.float32)
    for padded in (padded_d, padded_h):
        padded[:, 0:2] = zero_edge
        padded[:, nx + 2 : nx + 4] = zero_edge
        padded[:, :, 0:MARGIN] = jnp.zeros((2, nx + 4, MARGIN, nz), jnp.float32)
        padded[:, :, ny + MARGIN : ny + 2 * MARGIN] = jnp.zeros((2, nx + 4, MARGIN, nz), jnp.float32)

    def place_orbital(offset, part, block):
        x0, y0 = corner(offset)
        padded_d[part, pl.ds(x0 + 2, bx), pl.ds(y0 + MARGIN, by), :] = block
        evolved[part, pl.ds(x0, bx), pl.ds(y0, by), :] = block

    def place_potential(offset, block):
        x0, y0 = corner(offset)
        d = HALF_STEP * (DIAGONAL + block)
        diag[pl.ds(x0, bx), pl.ds(y0, by), :] = d
        inv[pl.ds(x0, bx), pl.ds(y0, by), :] = K2 / (1.0 + d * d)

    mine = jnp.minimum(layout.solved_by(here), layout.count - 1)
    place_potential(near[0], potential_ref[...])
    for offset, ref in zip(across, pots):
        place_potential(offset, ref[...])
    for part in range(2):
        place_orbital(near[0], part, orbitals_ref[part, mine])
    for (da, _, dc), ref in zip(near[1:], near_refs):
        for ds in range(layout.segments):
            place_potential((da, ds, dc), ref[2 + ds])
        for part in range(2):
            place_orbital((da, 0, dc), part, ref[part])
    for offset, ref in zip(far, far_refs):
        for part in range(2):
            place_orbital(offset, part, ref[part])

    apart = jnp.abs(lax.broadcasted_iota(jnp.int32, (2 * nz, nz), 0) % nz - lax.broadcasted_iota(jnp.int32, (2 * nz, nz), 1))
    weights = jnp.where(apart == 1, -RATIO, jnp.where(apart == 2, 1.0, 0.0)).astype(jnp.bfloat16)

    def along_z(center):
        high = center.astype(jnp.bfloat16)
        low = (center - high.astype(jnp.float32)).astype(jnp.bfloat16)
        return jnp.dot(jnp.concatenate([high, low], axis=1), weights, preferred_element_type=jnp.float32)

    def stencils(padded, x):
        rows = pl.ds(MARGIN, ny)
        flat = [padded[part, pl.ds(x + 2, planes), rows, :].reshape(planes * ny, nz) for part in range(2)]
        deep = along_z(jnp.concatenate(flat, axis=0))

        def at(part, i):
            def ring(s):
                return (padded[part, x + i + 2 + s, rows, :] + padded[part, x + i + 2 - s, rows, :]) + (
                    padded[part, x + i + 2, MARGIN + s : MARGIN + s + ny, :]
                    + padded[part, x + i + 2, MARGIN - s : MARGIN - s + ny, :]
                )

            start = (part * planes + i) * ny
            return (ring(2) - RATIO * ring(1)) + deep[start : start + ny]

        return [[at(part, i) for i in range(planes)] for part in range(2)]

    def over_planes(padded, at, acc):
        def step(i, acc):
            base = i * planes
            re, im = stencils(padded, base)
            for k in range(planes):
                acc = at(base + k, re[k], im[k], acc)
            return acc

        return lax.fori_loop(0, nx // planes, step, acc)

    def sums(count):
        return tuple(jnp.zeros((8, nz), jnp.float32) for _ in range(count))

    def precondition_at(re, im, x):
        d, scale = (diag[x], inv[x])
        return (re + d * im) * scale, (im - d * re) * scale

    def start(x, off_re, off_im, acc):
        d = diag[x]
        center_re = padded_d[0, x + 2, MARGIN : MARGIN + ny, :]
        center_im = padded_d[1, x + 2, MARGIN : MARGIN + ny, :]
        re = 2.0 * (d * center_im + K2 * off_im)
        im = -2.0 * (d * center_re + K2 * off_re)
        shadow[0, x] = re
        shadow[1, x] = im
        hat_re, hat_im = precondition_at(re, im, x)
        padded_h[0, x + 2, MARGIN : MARGIN + ny, :] = hat_re
        padded_h[1, x + 2, MARGIN : MARGIN + ny, :] = hat_im
        return (acc[0] + fold(re * re + im * im),)

    (norm,) = over_planes(padded_d, start, sums(1))
    rho = (total(norm), jnp.zeros((1, 1), jnp.float32))
    residual, direction = (shadow, shadow)
    hat, other = (padded_h, padded_d)

    for iteration in range(ITERS):

        def image_at(x, off_re, off_im, acc):
            re = direction[0, x] - off_im
            im = direction[1, x] + off_re
            image[0, x] = re
            image[1, x] = im
            s_re, s_im = (shadow[0, x], shadow[1, x])
            return (acc[0] + fold(s_re * re + s_im * im), acc[1] + fold(s_re * im - s_im * re))

        acc = over_planes(hat, image_at, sums(2))
        sigma = (total(acc[0]), total(acc[1]))
        alpha = divide_complex(rho, sigma)

        def half_at(x, acc):
            i_re, i_im = (image[0, x], image[1, x])
            re = residual[0, x] - (alpha[0] * i_re - alpha[1] * i_im)
            im = residual[1, x] - (alpha[0] * i_im + alpha[1] * i_re)
            res[0, x] = re
            res[1, x] = im
            hat_re, hat_im = precondition_at(re, im, x)
            other[0, x + 2, MARGIN : MARGIN + ny, :] = hat_re
            other[1, x + 2, MARGIN : MARGIN + ny, :] = hat_im
            s_re, s_im = (shadow[0, x], shadow[1, x])
            return (acc[0] + fold(s_re * re + s_im * im), acc[1] + fold(s_re * im - s_im * re))

        acc = lax.fori_loop(0, nx, half_at, sums(2), unroll=4)
        shadow_half = (total(acc[0]), total(acc[1]))

        def second_at(x, off_re, off_im, acc):
            h_re, h_im = (res[0, x], res[1, x])
            re = h_re - off_im
            im = h_im + off_re
            second[0, x] = re
            second[1, x] = im
            s_re, s_im = (shadow[0, x], shadow[1, x])
            return (
                acc[0] + fold(re * h_re + im * h_im),
                acc[1] + fold(re * h_im - im * h_re),
                acc[2] + fold(re * re + im * im),
                acc[3] + fold(s_re * re + s_im * im),
                acc[4] + fold(s_re * im - s_im * re),
            )

        acc = over_planes(other, second_at, sums(5))
        cross_re, cross_im, norm, ss_re, ss_im = [total(part) for part in acc]
        omega = (cross_re / norm, cross_im / norm)
        alpha_hat = (alpha[0] * (1.0 / K2), alpha[1] * (1.0 / K2))
        omega_hat = (omega[0] * (1.0 / K2), omega[1] * (1.0 / K2))

        def step_evolved(base, at_d, at_h):
            along_d = complex_mul(alpha_hat, at_d)
            along_h = complex_mul(omega_hat, at_h)
            return (base[0] + (along_d[0] + along_h[0]), base[1] + (along_d[1] + along_h[1]))

        if iteration + 1 < ITERS:
            moved = complex_mul(omega, (ss_re, ss_im))
            rho_next = (shadow_half[0] - moved[0], shadow_half[1] - moved[1])
            beta = complex_mul(divide_complex(rho_next, rho), divide_complex(alpha, omega))
            beta_omega = complex_mul(beta, omega)
            rho = rho_next

            def update_at(x, carry):
                at_d = (hat[0, x + 2, MARGIN : MARGIN + ny, :], hat[1, x + 2, MARGIN : MARGIN + ny, :])
                at_h = (other[0, x + 2, MARGIN : MARGIN + ny, :], other[1, x + 2, MARGIN : MARGIN + ny, :])
                e = step_evolved((evolved[0, x], evolved[1, x]), at_d, at_h)
                evolved[0, x] = e[0]
                evolved[1, x] = e[1]
                w = complex_mul(omega, (second[0, x], second[1, x]))
                r_re = res[0, x] - w[0]
                r_im = res[1, x] - w[1]
                res[0, x] = r_re
                res[1, x] = r_im
                p = complex_mul(beta, (direction[0, x], direction[1, x]))
                v = complex_mul(beta_omega, (image[0, x], image[1, x]))
                p_re = r_re + (p[0] - v[0])
                p_im = r_im + (p[1] - v[1])
                direc[0, x] = p_re
                direc[1, x] = p_im
                hat_re, hat_im = precondition_at(p_re, p_im, x)
                hat[0, x + 2, MARGIN : MARGIN + ny, :] = hat_re
                hat[1, x + 2, MARGIN : MARGIN + ny, :] = hat_im
                return carry

            lax.fori_loop(0, nx, update_at, 0, unroll=4)
            residual, direction = (res, direc)
        else:
            own = lax.axis_index("gx") * layout.columns + lax.axis_index("gyz")
            targets = [own] + [
                layout.looked_up({(m[0], m[1]): m[2][0] * layout.columns + m[2][1] for m in r}) for r in rounds
            ]
            for target, out in zip(targets, outs):
                x0 = target // layout.columns * bx
                y0 = pl.multiple_of(lax.rem(target, layout.columns) * by, 8)

                def finish_at(i, carry):
                    x, y = (x0 + i, pl.ds(y0, by))
                    yp = pl.ds(y0 + MARGIN, by)
                    at_d = (hat[0, x + 2, yp, :], hat[1, x + 2, yp, :])
                    at_h = (other[0, x + 2, yp, :], other[1, x + 2, yp, :])
                    e = step_evolved((evolved[0, x, y, :], evolved[1, x, y, :]), at_d, at_h)
                    w = complex_mul(omega, (second[0, x, y, :], second[1, x, y, :]))
                    out[0, i] = e[0]
                    out[1, i] = e[1]
                    out[2, i] = res[0, x, y, :] - w[0]
                    out[3, i] = res[1, x, y, :] - w[1]
                    return carry

                @pl.when(target >= 0)
                def _():
                    lax.fori_loop(0, bx, finish_at, 0, unroll=4)


def unpack_kernel(layout, *refs):
    rounds = layout.deliveries()
    blocks, (evolved_ref, residual_ref) = (refs[: 1 + len(rounds)], refs[1 + len(rounds) :])
    mine = layout.solved_by(layout.here())
    orbitals = [jnp.where(mine < layout.count, mine, -1)]
    orbitals += [layout.looked_up({(m[0], m[2]): m[3] for m in r}) for r in rounds]
    for q, block in zip(orbitals, blocks):

        @pl.when(q >= 0)
        def _():
            for part in range(2):
                evolved_ref[part, q] = block[part]
                residual_ref[part, q] = block[2 + part]


VMEM_SPEC = pl.BlockSpec(memory_space=pltpu.VMEM)


def whole_call(kernel, operands, out_shapes, limit, scratch=()):
    return pl.pallas_call(
        kernel,
        out_shape=[jax.ShapeDtypeStruct(dims, jnp.float32) for dims in out_shapes],
        in_specs=[VMEM_SPEC] * len(operands),
        out_specs=[VMEM_SPEC] * len(out_shapes),
        scratch_shapes=list(scratch),
        compiler_params=pltpu.CompilerParams(vmem_limit_bytes=limit),
    )(*operands)


def solve_scratch(nx, ny, nz):
    field = pltpu.VMEM((2, nx, ny, nz), jnp.float32)
    padded = pltpu.VMEM((2, nx + 4, ny + 2 * MARGIN, nz), jnp.float32)
    scalar_field = pltpu.VMEM((nx, ny, nz), jnp.float32)
    return [scalar_field] * 2 + [padded] * 2 + [field] * 6


def gathered(layout, orbitals, potential):
    _, _, bx, by, nz = orbitals.shape
    axes = ("orb", "gx", "gyz")
    near, far, across = (layout.near, layout.far, layout.across)
    slots = 2 + layout.segments

    def fetch(array, offset, to_owner):
        return lax.ppermute(array, axes, layout.pairs(offset, to_owner))

    pots = [fetch(potential, offset, False) for offset in across]
    far_messages = whole_call(
        functools.partial(pack_far_kernel, layout), [orbitals], [(2, bx, by, nz)] * len(far), 4 * 2**20
    )
    far_blocks = [fetch(message, offset, True) for offset, message in zip(far, far_messages)]
    near_messages = whole_call(
        functools.partial(pack_near_kernel, layout),
        [orbitals, potential] + pots,
        [(slots, bx, by, nz)] * (len(near) - 1),
        4 * 2**20,
    )
    near_blocks = [fetch(message, offset, True) for offset, message in zip(near[1:], near_messages)]
    rounds = layout.deliveries()
    pieces = whole_call(
        functools.partial(solve_kernel, layout),
        [orbitals, potential] + pots + near_blocks + far_blocks,
        [(4, bx, by, nz)] * (1 + len(rounds)),
        28 * 2**20,
        solve_scratch(bx * layout.rows, by * layout.columns, nz),
    )
    arrived = [pieces[0]]
    for messages, piece in zip(rounds, pieces[1:]):
        pairs = [
            ((g * layout.rows + s[0]) * layout.columns + s[1], (g * layout.rows + d[0]) * layout.columns + d[1])
            for g in range(layout.groups)
            for parity, s, d, _ in messages
            if g % 2 == parity
        ]
        arrived.append(lax.ppermute(piece, axes, pairs))
    return whole_call(functools.partial(unpack_kernel, layout), arrived, [orbitals.shape] * 2, 6 * 2**20)


def solution(mesh):
    sizes = dict(mesh.shape)

    def shards(orbitals, potential):
        _, count, bx, by, nz = orbitals.shape
        layout = Layout(sizes["orb"], sizes["gx"], sizes["gyz"], count)
        nx, ny = (bx * layout.rows, by * layout.columns)
        fields = 24 * 4 * (nx + 4) * (ny + 2 * MARGIN) * nz
        if layout.fits and fields <= WORKING_SET and by % 8 == 0 and nz % 128 == 0:
            return tuple(gathered(layout, orbitals, potential))
        return distributed(orbitals, potential)

    return jax.shard_map(
        shards,
        mesh=mesh,
        in_specs=(P(None, "orb", "gx", "gyz", None), P("gx", "gyz", None)),
        out_specs=(P(None, "orb", "gx", "gyz", None), P(None, "orb", "gx", "gyz", None)),
        check_vma=False,
    )
```

profile of v0, /device:TPU:0, one launch (start us, length us, event | category | flops | bytes accessed | tf_op | source)
XLA Modules:
  0.0 68.1 jit_solution(8626559144804350047)
XLA Ops:
  0.6 4.1 %collective-permute-start = (f32[16,8,128]{2,1,0:T(8,128)}, f32[16,8,128]{2,1,0:T(8,128)S(1)}, u32[]{:S(2)}, u32[]{:S(2)}) collective-permute-start(f32[16,8,128]{2,1,0:T(8,128)} %refs_1_.1), channel_id=1, source_target_pairs={{2,0},{3,1},{0,2},{1,3},{6,4},{7,5},{4,6},{5,7},{10,8},{11,9},{8,1... | collective-permute-start | bytes 196616 | tf_op jit(solution)/shard_map/ppermute | solution.py:553
  4.8 0.0 copy-start
  4.8 1.0 %copy-done = f32[2,3,16,8,128]{4,3,2,1,0:T(8,128)S(1)} copy-done((f32[2,3,16,8,128]{4,3,2,1,0:T(8,128)S(1)}, f32[2,3,16,8,128]{4,3,2,1,0:T(8,128)}, u32[]{:S(2)}) %copy-start) | copy-done | bytes 393240
  5.8 0.0 copy-start.1
  5.8 2.1 %collective-permute-start.4 = (f32[2,16,8,128]{3,2,1,0:T(8,128)S(1)}, f32[2,16,8,128]{3,2,1,0:T(8,128)S(1)}, u32[]{:S(2)}, u32[]{:S(2)}) collective-permute-start(f32[2,16,8,128]{3,2,1,0:T(8,128)S(1)} %get-tuple-element.17), channel_id=1, source_target_pairs={{2,0},{3,1},{0,2},{6,4},{4,6},{5,7},{11,9},{8,10},{9,11},{14,12},{... | collective-permute-start | bytes 393224 | tf_op jit(solution)/shard_map/ppermute | solution.py:553
  7.9 1.3 %collective-permute-start.5 = (f32[2,16,8,128]{3,2,1,0:T(8,128)S(1)}, f32[2,16,8,128]{3,2,1,0:T(8,128)S(1)}, u32[]{:S(2)}, u32[]{:S(2)}) collective-permute-start(f32[2,16,8,128]{3,2,1,0:T(8,128)S(1)} %get-tuple-element.18), channel_id=1, source_target_pairs={{3,0},{2,1},{1,2},{7,4},{5,6},{4,7},{10,9},{9,10},{8,11},{15,12},{... | collective-permute-start | bytes 393224 | tf_op jit(solution)/shard_map/ppermute | solution.py:553
  9.2 0.0 collective-permute-done.refs_0_.refs_2_
  9.2 0.0 copy-start.2
  9.2 0.8 %copy-done.2 = f32[16,8,128]{2,1,0:T(8,128)S(1)} copy-done((f32[16,8,128]{2,1,0:T(8,128)S(1)}, f32[16,8,128]{2,1,0:T(8,128)}, u32[]{:S(2)}) %copy-start.2) | copy-done | bytes 65560
  10.0 0.0 copy-start.3
  10.0 0.1 shard_map.41
  10.1 6.0 %collective-permute-start.1 = (f32[4,16,8,128]{3,2,1,0:T(8,128)S(1)}, f32[4,16,8,128]{3,2,1,0:T(8,128)S(1)}, u32[]{:S(2)}, u32[]{:S(2)}) collective-permute-start(f32[4,16,8,128]{3,2,1,0:T(8,128)S(1)} %get-tuple-element.14), channel_id=1, source_target_pairs={{1,0},{0,1},{3,2},{5,4},{7,6},{6,7},{8,9},{11,10},{10,11},{13,12},... | collective-permute-start | bytes 786440 | tf_op jit(solution)/shard_map/ppermute | solution.py:553
  16.1 1.9 %collective-permute-start.2 = (f32[4,16,8,128]{3,2,1,0:T(8,128)S(1)}, f32[4,16,8,128]{3,2,1,0:T(8,128)S(1)}, u32[]{:S(2)}, u32[]{:S(2)}) collective-permute-start(f32[4,16,8,128]{3,2,1,0:T(8,128)S(1)} %get-tuple-element.15), channel_id=1, source_target_pairs={{4,0},{5,1},{6,2},{0,4},{2,6},{3,7},{13,9},{14,10},{15,11},{8,12},... | collective-permute-start | bytes 786440 | tf_op jit(solution)/shard_map/ppermute | solution.py:553
  18.0 1.3 %collective-permute-start.3 = (f32[4,16,8,128]{3,2,1,0:T(8,128)S(1)}, f32[4,16,8,128]{3,2,1,0:T(8,128)S(1)}, u32[]{:S(2)}, u32[]{:S(2)}) collective-permute-start(f32[4,16,8,128]{3,2,1,0:T(8,128)S(1)} %get-tuple-element.16), channel_id=1, source_target_pairs={{5,0},{4,1},{7,2},{1,4},{3,6},{2,7},{12,9},{15,10},{14,11},{9,12},... | collective-permute-start | bytes 786440 | tf_op jit(solution)/shard_map/ppermute | solution.py:553
  19.3 0.0 collective-permute-done.4.refs_6_
  19.3 4.1 %collective-permute-start.6 = (f32[2,16,8,128]{3,2,1,0:T(8,128)S(1)}, f32[2,16,8,128]{3,2,1,0:T(8,128)S(1)}, u32[]{:S(2)}, u32[]{:S(2)}) collective-permute-start(f32[2,16,8,128]{3,2,1,0:T(8,128)S(1)} %get-tuple-element.19), channel_id=1, source_target_pairs={{6,0},{7,1},{4,2},{2,4},{0,6},{1,7},{15,9},{12,10},{13,11},{10,12}... | collective-permute-start | bytes 393224 | tf_op jit(solution)/shard_map/ppermute | solution.py:553
  23.4 0.0 collective-permute-done.5.refs_7_
  23.4 7.1 %collective-permute-start.7 = (f32[2,16,8,128]{3,2,1,0:T(8,128)S(1)}, f32[2,16,8,128]{3,2,1,0:T(8,128)S(1)}, u32[]{:S(2)}, u32[]{:S(2)}) collective-permute-start(f32[2,16,8,128]{3,2,1,0:T(8,128)S(1)} %get-tuple-element.20), channel_id=1, source_target_pairs={{7,0},{6,1},{5,2},{3,4},{1,6},{0,7},{14,9},{13,10},{12,11},{11,12}... | collective-permute-start | bytes 393224 | tf_op jit(solution)/shard_map/ppermute | solution.py:553
  30.5 0.0 collective-permute-done.6.refs_8_
  30.5 4.2 %collective-permute-done.7.refs_9_ = f32[2,16,8,128]{3,2,1,0:T(8,128)S(1)} collective-permute-done((f32[2,16,8,128]{3,2,1,0:T(8,128)S(1)}, f32[2,16,8,128]{3,2,1,0:T(8,128)S(1)}, u32[]{:S(2)}, u32[]{:S(2)}) %collective-permute-start.7) | collective-permute-done | bytes 131104 | tf_op jit(solution)/shard_map/ppermute | solution.py:553
  34.7 0.0 collective-permute-done.1.refs_3_
  34.7 1.2 %collective-permute-done.2.refs_4_ = f32[4,16,8,128]{3,2,1,0:T(8,128)S(1)} collective-permute-done((f32[4,16,8,128]{3,2,1,0:T(8,128)S(1)}, f32[4,16,8,128]{3,2,1,0:T(8,128)S(1)}, u32[]{:S(2)}, u32[]{:S(2)}) %collective-permute-start.2) | collective-permute-done | bytes 262176 | tf_op jit(solution)/shard_map/ppermute | solution.py:553
  35.9 0.0 collective-permute-done.3.refs_5_
  35.9 0.0 copy-done.1
  35.9 0.0 copy-done.3
  35.9 13.2 %shard_map.43 = (f32[4,16,8,128]{3,2,1,0:T(8,128)S(1)}, f32[4,16,8,128]{3,2,1,0:T(8,128)S(1)}, f32[4,16,8,128]{3,2,1,0:T(8,128)S(1)}, f32[4,16,8,128]{3,2,1,0:T(8,128)S(1)}, f32[4,16,8,128]{3,2,1,0:T(8,128)S(1)}) custom-call(f32[2,3,16,8,128]{4,3,2,1,0:T(8,128)S(1)} %copy-done.1, f32[16,8,128]{2,1,0:T(8,128)S(1)} %copy-done.3, ...), custom_call_target="tpu_custom_call" | custom-call | tf_op jit(solution)/shard_map/pallas_call | solution.py:529
  49.1 0.7 collective-permute-start.8
  49.8 1.3 %collective-permute-start.9 = (f32[4,16,8,128]{3,2,1,0:T(8,128)S(1)}, f32[4,16,8,128]{3,2,1,0:T(8,128)S(1)}, u32[]{:S(2)}, u32[]{:S(2)}) collective-permute-start(f32[4,16,8,128]{3,2,1,0:T(8,128)S(1)} %get-tuple-element.23), channel_id=1, source_target_pairs={{1,0},{2,1},{6,5},{7,6},{9,8},{10,9},{11,10},{13,12},{15,14},{17,1... | collective-permute-start | bytes 786440 | tf_op jit(solution)/shard_map/ppermute | solution.py:583
  51.1 7.7 %collective-permute-start.10 = (f32[4,16,8,128]{3,2,1,0:T(8,128)S(1)}, f32[4,16,8,128]{3,2,1,0:T(8,128)S(1)}, u32[]{:S(2)}, u32[]{:S(2)}) collective-permute-start(f32[4,16,8,128]{3,2,1,0:T(8,128)S(1)} %get-tuple-element.24), channel_id=1, source_target_pairs={{0,1},{1,2},{2,3},{4,5},{6,7},{9,10},{10,11},{12,13},{13,14},{16,1... | collective-permute-start | bytes 786440 | tf_op jit(solution)/shard_map/ppermute | solution.py:583
  58.9 1.9 %collective-permute-start.11 = (f32[4,16,8,128]{3,2,1,0:T(8,128)S(1)}, f32[4,16,8,128]{3,2,1,0:T(8,128)S(1)}, u32[]{:S(2)}, u32[]{:S(2)}) collective-permute-start(f32[4,16,8,128]{3,2,1,0:T(8,128)S(1)} %get-tuple-element.25), channel_id=1, source_target_pairs={{4,0},{6,2},{7,3},{0,4},{1,5},{2,6},{12,8},{13,9},{15,11},{9,13},{... | collective-permute-start | bytes 786440 | tf_op jit(solution)/shard_map/ppermute | solution.py:583
  60.8 0.0 collective-permute-done.8.refs_1_
  60.8 6.1 %collective-permute-done.9.refs_2_ = f32[4,16,8,128]{3,2,1,0:T(8,128)S(1)} collective-permute-done((f32[4,16,8,128]{3,2,1,0:T(8,128)S(1)}, f32[4,16,8,128]{3,2,1,0:T(8,128)S(1)}, u32[]{:S(2)}, u32[]{:S(2)}) %collective-permute-start.9) | collective-permute-done | bytes 262176 | tf_op jit(solution)/shard_map/ppermute | solution.py:583
  66.9 0.0 collective-permute-done.10.refs_3_
  66.9 0.2 collective-permute-done.11.refs_4_
  67.1 0.9 %shard_map.44 = (f32[2,3,16,8,128]{4,3,2,1,0:T(8,128)}, f32[2,3,16,8,128]{4,3,2,1,0:T(8,128)}) custom-call(f32[4,16,8,128]{3,2,1,0:T(8,128)S(1)} %get-tuple-element.21.refs_0_, f32[4,16,8,128]{3,2,1,0:T(8,128)S(1)} %collective-permute-done.8.refs_1_, f32[4,16,8,128]{3,2,1,0:T(8,128)S(1)} %collective-permute-done.9.refs_2_, ...), custom_call_target="tpu_custom_call" | custom-call | tf_op jit(solution)/shard_map/pallas_call | solution.py:529
  (1 shorter events, 0.0 us)
Async XLA Ops:
  0.6 8.5 %collective-permute-start = (f32[16,8,128]{2,1,0:T(8,128)}, f32[16,8,128]{2,1,0:T(8,128)S(1)}, u32[]{:S(2)}, u32[]{:S(2)}) collective-permute-start(f32[16,8,128]{2,1,0:T(8,128)} %refs_1_.1), channel_id=1, source_target_pairs={{2,0},{3,1},{0,2},{1,3},{6,4},{7,5},{4,6},{5,7},{10,8},{11,9},{8,1... | collective-permute-start | bytes 196616 | tf_op jit(solution)/shard_map/ppermute | solution.py:553
  4.8 1.0 %copy-start = (f32[2,3,16,8,128]{4,3,2,1,0:T(8,128)S(1)}, f32[2,3,16,8,128]{4,3,2,1,0:T(8,128)}, u32[]{:S(2)}) copy-start(f32[2,3,16,8,128]{4,3,2,1,0:T(8,128)} %refs_0_.1) | copy-start | bytes 1179652
  5.8 30.2 %copy-start.1 = (f32[2,3,16,8,128]{4,3,2,1,0:T(8,128)S(1)}, f32[2,3,16,8,128]{4,3,2,1,0:T(8,128)}, u32[]{:S(2)}) copy-start(f32[2,3,16,8,128]{4,3,2,1,0:T(8,128)} %refs_0_.1) | copy-start | bytes 1179652
  5.8 13.5 %collective-permute-start.4 = (f32[2,16,8,128]{3,2,1,0:T(8,128)S(1)}, f32[2,16,8,128]{3,2,1,0:T(8,128)S(1)}, u32[]{:S(2)}, u32[]{:S(2)}) collective-permute-start(f32[2,16,8,128]{3,2,1,0:T(8,128)S(1)} %get-tuple-element.17), channel_id=1, source_target_pairs={{2,0},{3,1},{0,2},{6,4},{4,6},{5,7},{11,9},{8,10},{9,11},{14,12},{... | collective-permute-start | bytes 393224 | tf_op jit(solution)/shard_map/ppermute | solution.py:553
  7.9 15.6 %collective-permute-start.5 = (f32[2,16,8,128]{3,2,1,0:T(8,128)S(1)}, f32[2,16,8,128]{3,2,1,0:T(8,128)S(1)}, u32[]{:S(2)}, u32[]{:S(2)}) collective-permute-start(f32[2,16,8,128]{3,2,1,0:T(8,128)S(1)} %get-tuple-element.18), channel_id=1, source_target_pairs={{3,0},{2,1},{1,2},{7,4},{5,6},{4,7},{10,9},{9,10},{8,11},{15,12},{... | collective-permute-start | bytes 393224 | tf_op jit(solution)/shard_map/ppermute | solution.py:553
  9.2 0.8 %copy-start.2 = (f32[16,8,128]{2,1,0:T(8,128)S(1)}, f32[16,8,128]{2,1,0:T(8,128)}, u32[]{:S(2)}) copy-start(f32[16,8,128]{2,1,0:T(8,128)} %refs_1_.1) | copy-start | bytes 196612
  10.0 25.9 %copy-start.3 = (f32[16,8,128]{2,1,0:T(8,128)S(1)}, f32[16,8,128]{2,1,0:T(8,128)}, u32[]{:S(2)}) copy-start(f32[16,8,128]{2,1,0:T(8,128)} %refs_1_.1) | copy-start | bytes 196612
  10.1 24.6 %collective-permute-start.1 = (f32[4,16,8,128]{3,2,1,0:T(8,128)S(1)}, f32[4,16,8,128]{3,2,1,0:T(8,128)S(1)}, u32[]{:S(2)}, u32[]{:S(2)}) collective-permute-start(f32[4,16,8,128]{3,2,1,0:T(8,128)S(1)} %get-tuple-element.14), channel_id=1, source_target_pairs={{1,0},{0,1},{3,2},{5,4},{7,6},{6,7},{8,9},{11,10},{10,11},{13,12},... | collective-permute-start | bytes 786440 | tf_op jit(solution)/shard_map/ppermute | solution.py:553
  16.1 19.8 %collective-permute-start.2 = (f32[4,16,8,128]{3,2,1,0:T(8,128)S(1)}, f32[4,16,8,128]{3,2,1,0:T(8,128)S(1)}, u32[]{:S(2)}, u32[]{:S(2)}) collective-permute-start(f32[4,16,8,128]{3,2,1,0:T(8,128)S(1)} %get-tuple-element.15), channel_id=1, source_target_pairs={{4,0},{5,1},{6,2},{0,4},{2,6},{3,7},{13,9},{14,10},{15,11},{8,12},... | collective-permute-start | bytes 786440 | tf_op jit(solution)/shard_map/ppermute | solution.py:553
  18.0 17.9 %collective-permute-start.3 = (f32[4,16,8,128]{3,2,1,0:T(8,128)S(1)}, f32[4,16,8,128]{3,2,1,0:T(8,128)S(1)}, u32[]{:S(2)}, u32[]{:S(2)}) collective-permute-start(f32[4,16,8,128]{3,2,1,0:T(8,128)S(1)} %get-tuple-element.16), channel_id=1, source_target_pairs={{5,0},{4,1},{7,2},{1,4},{3,6},{2,7},{12,9},{15,10},{14,11},{9,12},... | collective-permute-start | bytes 786440 | tf_op jit(solution)/shard_map/ppermute | solution.py:553
  19.3 11.2 %collective-permute-start.6 = (f32[2,16,8,128]{3,2,1,0:T(8,128)S(1)}, f32[2,16,8,128]{3,2,1,0:T(8,128)S(1)}, u32[]{:S(2)}, u32[]{:S(2)}) collective-permute-start(f32[2,16,8,128]{3,2,1,0:T(8,128)S(1)} %get-tuple-element.19), channel_id=1, source_target_pairs={{6,0},{7,1},{4,2},{2,4},{0,6},{1,7},{15,9},{12,10},{13,11},{10,12}... | collective-permute-start | bytes 393224 | tf_op jit(solution)/shard_map/ppermute | solution.py:553
  23.4 11.3 %collective-permute-start.7 = (f32[2,16,8,128]{3,2,1,0:T(8,128)S(1)}, f32[2,16,8,128]{3,2,1,0:T(8,128)S(1)}, u32[]{:S(2)}, u32[]{:S(2)}) collective-permute-start(f32[2,16,8,128]{3,2,1,0:T(8,128)S(1)} %get-tuple-element.20), channel_id=1, source_target_pairs={{7,0},{6,1},{5,2},{3,4},{1,6},{0,7},{14,9},{13,10},{12,11},{11,12}... | collective-permute-start | bytes 393224 | tf_op jit(solution)/shard_map/ppermute | solution.py:553
  49.1 11.7 %collective-permute-start.8 = (f32[4,16,8,128]{3,2,1,0:T(8,128)S(1)}, f32[4,16,8,128]{3,2,1,0:T(8,128)S(1)}, u32[]{:S(2)}, u32[]{:S(2)}) collective-permute-start(f32[4,16,8,128]{3,2,1,0:T(8,128)S(1)} %get-tuple-element.22), channel_id=1, source_target_pairs={{1,4},{6,3},{2,7},{13,8},{9,12},{10,15},{17,20},{22,19},{18,23},{2... | collective-permute-start | bytes 786440 | tf_op jit(solution)/shard_map/ppermute | solution.py:583
  49.8 17.1 %collective-permute-start.9 = (f32[4,16,8,128]{3,2,1,0:T(8,128)S(1)}, f32[4,16,8,128]{3,2,1,0:T(8,128)S(1)}, u32[]{:S(2)}, u32[]{:S(2)}) collective-permute-start(f32[4,16,8,128]{3,2,1,0:T(8,128)S(1)} %get-tuple-element.23), channel_id=1, source_target_pairs={{1,0},{2,1},{6,5},{7,6},{9,8},{10,9},{11,10},{13,12},{15,14},{17,1... | collective-permute-start | bytes 786440 | tf_op jit(solution)/shard_map/ppermute | solution.py:583
  51.1 15.8 %collective-permute-start.10 = (f32[4,16,8,128]{3,2,1,0:T(8,128)S(1)}, f32[4,16,8,128]{3,2,1,0:T(8,128)S(1)}, u32[]{:S(2)}, u32[]{:S(2)}) collective-permute-start(f32[4,16,8,128]{3,2,1,0:T(8,128)S(1)} %get-tuple-element.24), channel_id=1, source_target_pairs={{0,1},{1,2},{2,3},{4,5},{6,7},{9,10},{10,11},{12,13},{13,14},{16,1... | collective-permute-start | bytes 786440 | tf_op jit(solution)/shard_map/ppermute | solution.py:583
  58.9 8.3 %collective-permute-start.11 = (f32[4,16,8,128]{3,2,1,0:T(8,128)S(1)}, f32[4,16,8,128]{3,2,1,0:T(8,128)S(1)}, u32[]{:S(2)}, u32[]{:S(2)}) collective-permute-start(f32[4,16,8,128]{3,2,1,0:T(8,128)S(1)} %get-tuple-element.25), channel_id=1, source_target_pairs={{4,0},{6,2},{7,3},{0,4},{1,5},{2,6},{12,8},{13,9},{15,11},{9,13},{... | collective-permute-start | bytes 786440 | tf_op jit(solution)/shard_map/ppermute | solution.py:583
where the time goes:
time: 68.5 us; the launch traced here: 68.1 us
  starting transfers between devices  39.5 us (58%)
  Pallas kernels  14.2 us (21%)
  waiting for transfers between devices  11.7 us (17%)
  local copies, waits for them, and re-layouts  1.84 us (3%)
  between operations  0.79 us (1%)
    ppermute x8, starting transfers between devices, fetch(): return lax.ppermute(array, axes, layout.pairs(offset, to_owner))  27.9 us
    pallas_call x4, Pallas kernels, whole_call(): pl.pallas_call(kernel, out_shape=[jax.ShapeDtypeStruct(dims, jnp.float32)...  14.2 us
    ppermute x4, starting transfers between devices, gathered(): arrived.append(lax.ppermute(piece, axes, pairs))  11.6 us
    ppermute x4, waiting for transfers between devices, gathered(): arrived.append(lax.ppermute(piece, axes, pairs))  6.33 us
    ppermute x8, waiting for transfers between devices, fetch(): return lax.ppermute(array, axes, layout.pairs(offset, to_owner))  5.41 us
    unnamed x8, local copies, waits for them, and re-layouts  1.84 us
  transfers between devices with their start and end apart: 12, of which 4 were waited for; matrix products, arithmetic and copies ran while one was open for 0% of the time, Pallas kernels for 0%

commit v1 on v0

--- a/solution.py
+++ b/solution.py
@@ -210,10 +210,11 @@
                         continue
                     hops = lambda p: abs(p[0] - target[0]) + abs(p[1] - target[1])
                     source = min((p for p in places if owner[p] == q), key=hops)
-                    step = (target[0] != source[0], target[1] - source[1])
+                    swap = min(target[1], source[1]) % 2 if target[0] == source[0] else 0
+                    step = (target[0] != source[0], abs(target[1] - source[1]), swap)
                     classes.setdefault(step, []).append((parity, source, target, q))
         rounds = []
-        for step in sorted(classes, key=lambda s: (-int(s[0]) - abs(s[1]), s)):
+        for step in sorted(classes, key=lambda s: (s[2], s[0], -s[1])):
             for r in rounds:
                 busy = {(m[0], m[1], 0) for m in r} | {(m[0], m[2], 1) for m in r}
                 if not any((m[0], m[1], 0) in busy or (m[0], m[2], 1) in busy for m in classes[step]):

time: 68.5 us -> 67.3 us (0.982)
  starting transfers between devices: 39.5 us -> 35.7 us
  waiting for transfers between devices: 11.7 us -> 14.2 us
    ppermute x4, starting transfers between devices: 11.6 us -> 7.81 us  [gathered(): arrived.append(lax.ppermute(piece, axes, pairs))]
    ppermute x4, waiting for transfers between devices: 6.33 us -> 8.8 us  [gathered(): arrived.append(lax.ppermute(piece, axes, pairs))]
where the time goes in v1:
time: 67.3 us; the launch traced here: 66.7 us
  starting transfers between devices  35.7 us (53%)
  Pallas kernels  14.2 us (21%)
  waiting for transfers between devices  14.2 us (21%)
  local copies, waits for them, and re-layouts  1.84 us (3%)
  between operations  0.78 us (1%)
    ppermute x8, starting transfers between devices, fetch(): return lax.ppermute(array, axes, layout.pairs(offset, to_owner))  27.9 us
    pallas_call x4, Pallas kernels, whole_call(): pl.pallas_call(kernel, out_shape=[jax.ShapeDtypeStruct(dims, jnp.float32)...  14.2 us
    ppermute x4, waiting for transfers between devices, gathered(): arrived.append(lax.ppermute(piece, axes, pairs))  8.8 us
    ppermute x4, starting transfers between devices, gathered(): arrived.append(lax.ppermute(piece, axes, pairs))  7.81 us
    ppermute x8, waiting for transfers between devices, fetch(): return lax.ppermute(array, axes, layout.pairs(offset, to_owner))  5.41 us
    unnamed x8, local copies, waits for them, and re-layouts  1.84 us
  transfers between devices with their start and end apart: 12, of which 4 were waited for; matrix products, arithmetic and copies ran while one was open for 0% of the time, Pallas kernels for 0%

profile of v1, /device:TPU:0, one launch (start us, length us, event | category | flops | bytes accessed | tf_op | source)
XLA Modules:
  0.0 66.7 jit_solution(13118036996717383558)
XLA Ops:
  0.6 4.1 %collective-permute-start = (f32[16,8,128]{2,1,0:T(8,128)}, f32[16,8,128]{2,1,0:T(8,128)S(1)}, u32[]{:S(2)}, u32[]{:S(2)}) collective-permute-start(f32[16,8,128]{2,1,0:T(8,128)} %refs_1_.1), channel_id=1, source_target_pairs={{2,0},{3,1},{0,2},{1,3},{6,4},{7,5},{4,6},{5,7},{10,8},{11,9},{8,1... | collective-permute-start | bytes 196616 | tf_op jit(solution)/shard_map/ppermute | solution.py:554
  4.8 0.0 copy-start
  4.8 1.0 %copy-done = f32[2,3,16,8,128]{4,3,2,1,0:T(8,128)S(1)} copy-done((f32[2,3,16,8,128]{4,3,2,1,0:T(8,128)S(1)}, f32[2,3,16,8,128]{4,3,2,1,0:T(8,128)}, u32[]{:S(2)}) %copy-start) | copy-done | bytes 393240
  5.8 0.0 copy-start.1
  5.8 2.1 %collective-permute-start.4 = (f32[2,16,8,128]{3,2,1,0:T(8,128)S(1)}, f32[2,16,8,128]{3,2,1,0:T(8,128)S(1)}, u32[]{:S(2)}, u32[]{:S(2)}) collective-permute-start(f32[2,16,8,128]{3,2,1,0:T(8,128)S(1)} %get-tuple-element.17), channel_id=1, source_target_pairs={{2,0},{3,1},{0,2},{6,4},{4,6},{5,7},{11,9},{8,10},{9,11},{14,12},{... | collective-permute-start | bytes 393224 | tf_op jit(solution)/shard_map/ppermute | solution.py:554
  7.9 1.3 %collective-permute-start.5 = (f32[2,16,8,128]{3,2,1,0:T(8,128)S(1)}, f32[2,16,8,128]{3,2,1,0:T(8,128)S(1)}, u32[]{:S(2)}, u32[]{:S(2)}) collective-permute-start(f32[2,16,8,128]{3,2,1,0:T(8,128)S(1)} %get-tuple-element.18), channel_id=1, source_target_pairs={{3,0},{2,1},{1,2},{7,4},{5,6},{4,7},{10,9},{9,10},{8,11},{15,12},{... | collective-permute-start | bytes 393224 | tf_op jit(solution)/shard_map/ppermute | solution.py:554
  9.2 0.0 collective-permute-done.refs_0_.refs_2_
  9.2 0.0 copy-start.2
  9.2 0.8 %copy-done.2 = f32[16,8,128]{2,1,0:T(8,128)S(1)} copy-done((f32[16,8,128]{2,1,0:T(8,128)S(1)}, f32[16,8,128]{2,1,0:T(8,128)}, u32[]{:S(2)}) %copy-start.2) | copy-done | bytes 65560
  10.0 0.0 copy-start.3
  10.0 0.1 shard_map.41
  10.1 6.0 %collective-permute-start.1 = (f32[4,16,8,128]{3,2,1,0:T(8,128)S(1)}, f32[4,16,8,128]{3,2,1,0:T(8,128)S(1)}, u32[]{:S(2)}, u32[]{:S(2)}) collective-permute-start(f32[4,16,8,128]{3,2,1,0:T(8,128)S(1)} %get-tuple-element.14), channel_id=1, source_target_pairs={{1,0},{0,1},{3,2},{5,4},{7,6},{6,7},{8,9},{11,10},{10,11},{13,12},... | collective-permute-start | bytes 786440 | tf_op jit(solution)/shard_map/ppermute | solution.py:554
  16.1 1.9 %collective-permute-start.2 = (f32[4,16,8,128]{3,2,1,0:T(8,128)S(1)}, f32[4,16,8,128]{3,2,1,0:T(8,128)S(1)}, u32[]{:S(2)}, u32[]{:S(2)}) collective-permute-start(f32[4,16,8,128]{3,2,1,0:T(8,128)S(1)} %get-tuple-element.15), channel_id=1, source_target_pairs={{4,0},{5,1},{6,2},{0,4},{2,6},{3,7},{13,9},{14,10},{15,11},{8,12},... | collective-permute-start | bytes 786440 | tf_op jit(solution)/shard_map/ppermute | solution.py:554
  18.0 1.3 %collective-permute-start.3 = (f32[4,16,8,128]{3,2,1,0:T(8,128)S(1)}, f32[4,16,8,128]{3,2,1,0:T(8,128)S(1)}, u32[]{:S(2)}, u32[]{:S(2)}) collective-permute-start(f32[4,16,8,128]{3,2,1,0:T(8,128)S(1)} %get-tuple-element.16), channel_id=1, source_target_pairs={{5,0},{4,1},{7,2},{1,4},{3,6},{2,7},{12,9},{15,10},{14,11},{9,12},... | collective-permute-start | bytes 786440 | tf_op jit(solution)/shard_map/ppermute | solution.py:554
  19.3 0.0 collective-permute-done.4.refs_6_
  19.3 4.1 %collective-permute-start.6 = (f32[2,16,8,128]{3,2,1,0:T(8,128)S(1)}, f32[2,16,8,128]{3,2,1,0:T(8,128)S(1)}, u32[]{:S(2)}, u32[]{:S(2)}) collective-permute-start(f32[2,16,8,128]{3,2,1,0:T(8,128)S(1)} %get-tuple-element.19), channel_id=1, source_target_pairs={{6,0},{7,1},{4,2},{2,4},{0,6},{1,7},{15,9},{12,10},{13,11},{10,12}... | collective-permute-start | bytes 393224 | tf_op jit(solution)/shard_map/ppermute | solution.py:554
  23.4 0.0 collective-permute-done.5.refs_7_
  23.4 7.1 %collective-permute-start.7 = (f32[2,16,8,128]{3,2,1,0:T(8,128)S(1)}, f32[2,16,8,128]{3,2,1,0:T(8,128)S(1)}, u32[]{:S(2)}, u32[]{:S(2)}) collective-permute-start(f32[2,16,8,128]{3,2,1,0:T(8,128)S(1)} %get-tuple-element.20), channel_id=1, source_target_pairs={{7,0},{6,1},{5,2},{3,4},{1,6},{0,7},{14,9},{13,10},{12,11},{11,12}... | collective-permute-start | bytes 393224 | tf_op jit(solution)/shard_map/ppermute | solution.py:554
  30.5 0.0 collective-permute-done.6.refs_8_
  30.5 4.2 %collective-permute-done.7.refs_9_ = f32[2,16,8,128]{3,2,1,0:T(8,128)S(1)} collective-permute-done((f32[2,16,8,128]{3,2,1,0:T(8,128)S(1)}, f32[2,16,8,128]{3,2,1,0:T(8,128)S(1)}, u32[]{:S(2)}, u32[]{:S(2)}) %collective-permute-start.7) | collective-permute-done | bytes 131104 | tf_op jit(solution)/shard_map/ppermute | solution.py:554
  34.7 0.0 collective-permute-done.1.refs_3_
  34.7 1.2 %collective-permute-done.2.refs_4_ = f32[4,16,8,128]{3,2,1,0:T(8,128)S(1)} collective-permute-done((f32[4,16,8,128]{3,2,1,0:T(8,128)S(1)}, f32[4,16,8,128]{3,2,1,0:T(8,128)S(1)}, u32[]{:S(2)}, u32[]{:S(2)}) %collective-permute-start.2) | collective-permute-done | bytes 262176 | tf_op jit(solution)/shard_map/ppermute | solution.py:554
  35.9 0.0 collective-permute-done.3.refs_5_
  35.9 0.0 copy-done.1
  35.9 0.0 copy-done.3
  35.9 13.2 %shard_map.43 = (f32[4,16,8,128]{3,2,1,0:T(8,128)S(1)}, f32[4,16,8,128]{3,2,1,0:T(8,128)S(1)}, f32[4,16,8,128]{3,2,1,0:T(8,128)S(1)}, f32[4,16,8,128]{3,2,1,0:T(8,128)S(1)}, f32[4,16,8,128]{3,2,1,0:T(8,128)S(1)}) custom-call(f32[2,3,16,8,128]{4,3,2,1,0:T(8,128)S(1)} %copy-done.1, f32[16,8,128]{2,1,0:T(8,128)S(1)} %copy-done.3, ...), custom_call_target="tpu_custom_call" | custom-call | tf_op jit(solution)/shard_map/pallas_call | solution.py:530
  49.1 4.5 %collective-permute-start.8 = (f32[4,16,8,128]{3,2,1,0:T(8,128)S(1)}, f32[4,16,8,128]{3,2,1,0:T(8,128)S(1)}, u32[]{:S(2)}, u32[]{:S(2)}) collective-permute-start(f32[4,16,8,128]{3,2,1,0:T(8,128)S(1)} %get-tuple-element.22), channel_id=1, source_target_pairs={{1,0},{0,1},{2,3},{4,5},{7,6},{6,7},{9,8},{11,10},{10,11},{13,12},... | collective-permute-start | bytes 786440 | tf_op jit(solution)/shard_map/ppermute | solution.py:584
  53.7 0.7 %collective-permute-start.9 = (f32[4,16,8,128]{3,2,1,0:T(8,128)S(1)}, f32[4,16,8,128]{3,2,1,0:T(8,128)S(1)}, u32[]{:S(2)}, u32[]{:S(2)}) collective-permute-start(f32[4,16,8,128]{3,2,1,0:T(8,128)S(1)} %get-tuple-element.23), channel_id=1, source_target_pairs={{6,3},{1,4},{2,7},{13,8},{9,12},{10,15},{22,19},{17,20},{18,23},{2... | collective-permute-start | bytes 786440 | tf_op jit(solution)/shard_map/ppermute | solution.py:584
  54.4 1.9 %collective-permute-start.10 = (f32[4,16,8,128]{3,2,1,0:T(8,128)S(1)}, f32[4,16,8,128]{3,2,1,0:T(8,128)S(1)}, u32[]{:S(2)}, u32[]{:S(2)}) collective-permute-start(f32[4,16,8,128]{3,2,1,0:T(8,128)S(1)} %get-tuple-element.24), channel_id=1, source_target_pairs={{4,0},{6,2},{7,3},{0,4},{1,5},{2,6},{12,8},{13,9},{15,11},{9,13},{... | collective-permute-start | bytes 786440 | tf_op jit(solution)/shard_map/ppermute | solution.py:584
  56.3 0.7 %collective-permute-start.11 = (f32[4,16,8,128]{3,2,1,0:T(8,128)S(1)}, f32[4,16,8,128]{3,2,1,0:T(8,128)S(1)}, u32[]{:S(2)}, u32[]{:S(2)}) collective-permute-start(f32[4,16,8,128]{3,2,1,0:T(8,128)S(1)} %get-tuple-element.25), channel_id=1, source_target_pairs={{2,1},{1,2},{6,5},{10,9},{9,10},{13,14},{18,17},{17,18},{22,21},{2... | collective-permute-start | bytes 786440 | tf_op jit(solution)/shard_map/ppermute | solution.py:584
  57.0 3.8 %collective-permute-done.8.refs_1_ = f32[4,16,8,128]{3,2,1,0:T(8,128)S(1)} collective-permute-done((f32[4,16,8,128]{3,2,1,0:T(8,128)S(1)}, f32[4,16,8,128]{3,2,1,0:T(8,128)S(1)}, u32[]{:S(2)}, u32[]{:S(2)}) %collective-permute-start.8) | collective-permute-done | bytes 262176 | tf_op jit(solution)/shard_map/ppermute | solution.py:584
  60.8 0.0 collective-permute-done.9.refs_2_
  60.8 5.0 %collective-permute-done.10.refs_3_ = f32[4,16,8,128]{3,2,1,0:T(8,128)S(1)} collective-permute-done((f32[4,16,8,128]{3,2,1,0:T(8,128)S(1)}, f32[4,16,8,128]{3,2,1,0:T(8,128)S(1)}, u32[]{:S(2)}, u32[]{:S(2)}) %collective-permute-start.10) | collective-permute-done | bytes 262176 | tf_op jit(solution)/shard_map/ppermute | solution.py:584
  65.8 0.0 collective-permute-done.11.refs_4_
  65.8 0.9 %shard_map.44 = (f32[2,3,16,8,128]{4,3,2,1,0:T(8,128)}, f32[2,3,16,8,128]{4,3,2,1,0:T(8,128)}) custom-call(f32[4,16,8,128]{3,2,1,0:T(8,128)S(1)} %get-tuple-element.21.refs_0_, f32[4,16,8,128]{3,2,1,0:T(8,128)S(1)} %collective-permute-done.8.refs_1_, f32[4,16,8,128]{3,2,1,0:T(8,128)S(1)} %collective-permute-done.9.refs_2_, ...), custom_call_target="tpu_custom_call" | custom-call | tf_op jit(solution)/shard_map/pallas_call | solution.py:530
  (1 shorter events, 0.0 us)
Async XLA Ops:
  0.6 8.5 %collective-permute-start = (f32[16,8,128]{2,1,0:T(8,128)}, f32[16,8,128]{2,1,0:T(8,128)S(1)}, u32[]{:S(2)}, u32[]{:S(2)}) collective-permute-start(f32[16,8,128]{2,1,0:T(8,128)} %refs_1_.1), channel_id=1, source_target_pairs={{2,0},{3,1},{0,2},{1,3},{6,4},{7,5},{4,6},{5,7},{10,8},{11,9},{8,1... | collective-permute-start | bytes 196616 | tf_op jit(solution)/shard_map/ppermute | solution.py:554
  4.8 1.0 %copy-start = (f32[2,3,16,8,128]{4,3,2,1,0:T(8,128)S(1)}, f32[2,3,16,8,128]{4,3,2,1,0:T(8,128)}, u32[]{:S(2)}) copy-start(f32[2,3,16,8,128]{4,3,2,1,0:T(8,128)} %refs_0_.1) | copy-start | bytes 1179652
  5.8 30.2 %copy-start.1 = (f32[2,3,16,8,128]{4,3,2,1,0:T(8,128)S(1)}, f32[2,3,16,8,128]{4,3,2,1,0:T(8,128)}, u32[]{:S(2)}) copy-start(f32[2,3,16,8,128]{4,3,2,1,0:T(8,128)} %refs_0_.1) | copy-start | bytes 1179652
  5.8 13.5 %collective-permute-start.4 = (f32[2,16,8,128]{3,2,1,0:T(8,128)S(1)}, f32[2,16,8,128]{3,2,1,0:T(8,128)S(1)}, u32[]{:S(2)}, u32[]{:S(2)}) collective-permute-start(f32[2,16,8,128]{3,2,1,0:T(8,128)S(1)} %get-tuple-element.17), channel_id=1, source_target_pairs={{2,0},{3,1},{0,2},{6,4},{4,6},{5,7},{11,9},{8,10},{9,11},{14,12},{... | collective-permute-start | bytes 393224 | tf_op jit(solution)/shard_map/ppermute | solution.py:554
  7.9 15.6 %collective-permute-start.5 = (f32[2,16,8,128]{3,2,1,0:T(8,128)S(1)}, f32[2,16,8,128]{3,2,1,0:T(8,128)S(1)}, u32[]{:S(2)}, u32[]{:S(2)}) collective-permute-start(f32[2,16,8,128]{3,2,1,0:T(8,128)S(1)} %get-tuple-element.18), channel_id=1, source_target_pairs={{3,0},{2,1},{1,2},{7,4},{5,6},{4,7},{10,9},{9,10},{8,11},{15,12},{... | collective-permute-start | bytes 393224 | tf_op jit(solution)/shard_map/ppermute | solution.py:554
  9.2 0.8 %copy-start.2 = (f32[16,8,128]{2,1,0:T(8,128)S(1)}, f32[16,8,128]{2,1,0:T(8,128)}, u32[]{:S(2)}) copy-start(f32[16,8,128]{2,1,0:T(8,128)} %refs_1_.1) | copy-start | bytes 196612
  10.0 25.9 %copy-start.3 = (f32[16,8,128]{2,1,0:T(8,128)S(1)}, f32[16,8,128]{2,1,0:T(8,128)}, u32[]{:S(2)}) copy-start(f32[16,8,128]{2,1,0:T(8,128)} %refs_1_.1) | copy-start | bytes 196612
  10.1 24.6 %collective-permute-start.1 = (f32[4,16,8,128]{3,2,1,0:T(8,128)S(1)}, f32[4,16,8,128]{3,2,1,0:T(8,128)S(1)}, u32[]{:S(2)}, u32[]{:S(2)}) collective-permute-start(f32[4,16,8,128]{3,2,1,0:T(8,128)S(1)} %get-tuple-element.14), channel_id=1, source_target_pairs={{1,0},{0,1},{3,2},{5,4},{7,6},{6,7},{8,9},{11,10},{10,11},{13,12},... | collective-permute-start | bytes 786440 | tf_op jit(solution)/shard_map/ppermute | solution.py:554
  16.1 19.8 %collective-permute-start.2 = (f32[4,16,8,128]{3,2,1,0:T(8,128)S(1)}, f32[4,16,8,128]{3,2,1,0:T(8,128)S(1)}, u32[]{:S(2)}, u32[]{:S(2)}) collective-permute-start(f32[4,16,8,128]{3,2,1,0:T(8,128)S(1)} %get-tuple-element.15), channel_id=1, source_target_pairs={{4,0},{5,1},{6,2},{0,4},{2,6},{3,7},{13,9},{14,10},{15,11},{8,12},... | collective-permute-start | bytes 786440 | tf_op jit(solution)/shard_map/ppermute | solution.py:554
  18.0 17.9 %collective-permute-start.3 = (f32[4,16,8,128]{3,2,1,0:T(8,128)S(1)}, f32[4,16,8,128]{3,2,1,0:T(8,128)S(1)}, u32[]{:S(2)}, u32[]{:S(2)}) collective-permute-start(f32[4,16,8,128]{3,2,1,0:T(8,128)S(1)} %get-tuple-element.16), channel_id=1, source_target_pairs={{5,0},{4,1},{7,2},{1,4},{3,6},{2,7},{12,9},{15,10},{14,11},{9,12},... | collective-permute-start | bytes 786440 | tf_op jit(solution)/shard_map/ppermute | solution.py:554
  19.3 11.2 %collective-permute-start.6 = (f32[2,16,8,128]{3,2,1,0:T(8,128)S(1)}, f32[2,16,8,128]{3,2,1,0:T(8,128)S(1)}, u32[]{:S(2)}, u32[]{:S(2)}) collective-permute-start(f32[2,16,8,128]{3,2,1,0:T(8,128)S(1)} %get-tuple-element.19), channel_id=1, source_target_pairs={{6,0},{7,1},{4,2},{2,4},{0,6},{1,7},{15,9},{12,10},{13,11},{10,12}... | collective-permute-start | bytes 393224 | tf_op jit(solution)/shard_map/ppermute | solution.py:554
  23.4 11.3 %collective-permute-start.7 = (f32[2,16,8,128]{3,2,1,0:T(8,128)S(1)}, f32[2,16,8,128]{3,2,1,0:T(8,128)S(1)}, u32[]{:S(2)}, u32[]{:S(2)}) collective-permute-start(f32[2,16,8,128]{3,2,1,0:T(8,128)S(1)} %get-tuple-element.20), channel_id=1, source_target_pairs={{7,0},{6,1},{5,2},{3,4},{1,6},{0,7},{14,9},{13,10},{12,11},{11,12}... | collective-permute-start | bytes 393224 | tf_op jit(solution)/shard_map/ppermute | solution.py:554
  49.1 11.7 %collective-permute-start.8 = (f32[4,16,8,128]{3,2,1,0:T(8,128)S(1)}, f32[4,16,8,128]{3,2,1,0:T(8,128)S(1)}, u32[]{:S(2)}, u32[]{:S(2)}) collective-permute-start(f32[4,16,8,128]{3,2,1,0:T(8,128)S(1)} %get-tuple-element.22), channel_id=1, source_target_pairs={{1,0},{0,1},{2,3},{4,5},{7,6},{6,7},{9,8},{11,10},{10,11},{13,12},... | collective-permute-start | bytes 786440 | tf_op jit(solution)/shard_map/ppermute | solution.py:584
  53.7 7.1 %collective-permute-start.9 = (f32[4,16,8,128]{3,2,1,0:T(8,128)S(1)}, f32[4,16,8,128]{3,2,1,0:T(8,128)S(1)}, u32[]{:S(2)}, u32[]{:S(2)}) collective-permute-start(f32[4,16,8,128]{3,2,1,0:T(8,128)S(1)} %get-tuple-element.23), channel_id=1, source_target_pairs={{6,3},{1,4},{2,7},{13,8},{9,12},{10,15},{22,19},{17,20},{18,23},{2... | collective-permute-start | bytes 786440 | tf_op jit(solution)/shard_map/ppermute | solution.py:584
  54.4 11.4 %collective-permute-start.10 = (f32[4,16,8,128]{3,2,1,0:T(8,128)S(1)}, f32[4,16,8,128]{3,2,1,0:T(8,128)S(1)}, u32[]{:S(2)}, u32[]{:S(2)}) collective-permute-start(f32[4,16,8,128]{3,2,1,0:T(8,128)S(1)} %get-tuple-element.24), channel_id=1, source_target_pairs={{4,0},{6,2},{7,3},{0,4},{1,5},{2,6},{12,8},{13,9},{15,11},{9,13},{... | collective-permute-start | bytes 786440 | tf_op jit(solution)/shard_map/ppermute | solution.py:584
  56.3 9.5 %collective-permute-start.11 = (f32[4,16,8,128]{3,2,1,0:T(8,128)S(1)}, f32[4,16,8,128]{3,2,1,0:T(8,128)S(1)}, u32[]{:S(2)}, u32[]{:S(2)}) collective-permute-start(f32[4,16,8,128]{3,2,1,0:T(8,128)S(1)} %get-tuple-element.25), channel_id=1, source_target_pairs={{2,1},{1,2},{6,5},{10,9},{9,10},{13,14},{18,17},{17,18},{22,21},{2... | collective-permute-start | bytes 786440 | tf_op jit(solution)/shard_map/ppermute | solution.py:584

commit v2 on v1

--- a/solution.py
+++ b/solution.py
@@ -421,7 +421,7 @@
             s_re, s_im = (shadow[0, x], shadow[1, x])
             return (acc[0] + fold(s_re * re + s_im * im), acc[1] + fold(s_re * im - s_im * re))
 
-        acc = lax.fori_loop(0, nx, half_at, sums(2), unroll=4)
+        acc = lax.fori_loop(0, nx, half_at, sums(2), unroll=8)
         shadow_half = (total(acc[0]), total(acc[1]))
 
         def second_at(x, off_re, off_im, acc):
@@ -479,7 +479,7 @@
                 hat[1, x + 2, MARGIN : MARGIN + ny, :] = hat_im
                 return carry
 
-            lax.fori_loop(0, nx, update_at, 0, unroll=4)
+            lax.fori_loop(0, nx, update_at, 0, unroll=8)
             residual, direction = (res, direc)
         else:
             own = lax.axis_index("gx") * layout.columns + lax.axis_index("gyz")
@@ -505,7 +505,7 @@
 
                 @pl.when(target >= 0)
                 def _():
-                    lax.fori_loop(0, bx, finish_at, 0, unroll=4)
+                    lax.fori_loop(0, bx, finish_at, 0, unroll=8)
 
 
 def unpack_kernel(layout, *refs):

time: 67.3 us -> 67.2 us (level)
  no operation moved by 1% of the time
where the time goes in v2:
time: 67.2 us; the launch traced here: 66.5 us
  starting transfers between devices  35.6 us (53%)
  waiting for transfers between devices  14.2 us (21%)
  Pallas kernels  14.1 us (21%)
  local copies, waits for them, and re-layouts  1.84 us (3%)
  between operations  0.78 us (1%)
    ppermute x8, starting transfers between devices, fetch(): return lax.ppermute(array, axes, layout.pairs(offset, to_owner))  27.9 us
    pallas_call x4, Pallas kernels, whole_call(): pl.pallas_call(kernel, out_shape=[jax.ShapeDtypeStruct(dims, jnp.float32)...  14.1 us
    ppermute x4, waiting for transfers between devices, gathered(): arrived.append(lax.ppermute(piece, axes, pairs))  8.8 us
    ppermute x4, starting transfers between devices, gathered(): arrived.append(lax.ppermute(piece, axes, pairs))  7.79 us
    ppermute x8, waiting for transfers between devices, fetch(): return lax.ppermute(array, axes, layout.pairs(offset, to_owner))  5.41 us
    unnamed x8, local copies, waits for them, and re-layouts  1.84 us
  transfers between devices with their start and end apart: 12, of which 4 were waited for; matrix products, arithmetic and copies ran while one was open for 0% of the time, Pallas kernels for 0%

profile of v2, /device:TPU:0, one launch (start us, length us, event | category | flops | bytes accessed | tf_op | source)
XLA Modules:
  0.0 66.5 jit_solution(8835368812893606467)
XLA Ops:
  0.6 4.1 %collective-permute-start = (f32[16,8,128]{2,1,0:T(8,128)}, f32[16,8,128]{2,1,0:T(8,128)S(1)}, u32[]{:S(2)}, u32[]{:S(2)}) collective-permute-start(f32[16,8,128]{2,1,0:T(8,128)} %refs_1_.1), channel_id=1, source_target_pairs={{2,0},{3,1},{0,2},{1,3},{6,4},{7,5},{4,6},{5,7},{10,8},{11,9},{8,1... | collective-permute-start | bytes 196616 | tf_op jit(solution)/shard_map/ppermute | solution.py:554
  4.8 0.0 copy-start
  4.8 1.0 %copy-done = f32[2,3,16,8,128]{4,3,2,1,0:T(8,128)S(1)} copy-done((f32[2,3,16,8,128]{4,3,2,1,0:T(8,128)S(1)}, f32[2,3,16,8,128]{4,3,2,1,0:T(8,128)}, u32[]{:S(2)}) %copy-start) | copy-done | bytes 393240
  5.8 0.0 copy-start.1
  5.8 2.1 %collective-permute-start.4 = (f32[2,16,8,128]{3,2,1,0:T(8,128)S(1)}, f32[2,16,8,128]{3,2,1,0:T(8,128)S(1)}, u32[]{:S(2)}, u32[]{:S(2)}) collective-permute-start(f32[2,16,8,128]{3,2,1,0:T(8,128)S(1)} %get-tuple-element.17), channel_id=1, source_target_pairs={{2,0},{3,1},{0,2},{6,4},{4,6},{5,7},{11,9},{8,10},{9,11},{14,12},{... | collective-permute-start | bytes 393224 | tf_op jit(solution)/shard_map/ppermute | solution.py:554
  7.9 1.3 %collective-permute-start.5 = (f32[2,16,8,128]{3,2,1,0:T(8,128)S(1)}, f32[2,16,8,128]{3,2,1,0:T(8,128)S(1)}, u32[]{:S(2)}, u32[]{:S(2)}) collective-permute-start(f32[2,16,8,128]{3,2,1,0:T(8,128)S(1)} %get-tuple-element.18), channel_id=1, source_target_pairs={{3,0},{2,1},{1,2},{7,4},{5,6},{4,7},{10,9},{9,10},{8,11},{15,12},{... | collective-permute-start | bytes 393224 | tf_op jit(solution)/shard_map/ppermute | solution.py:554
  9.2 0.0 collective-permute-done.refs_0_.refs_2_
  9.2 0.0 copy-start.2
  9.2 0.8 %copy-done.2 = f32[16,8,128]{2,1,0:T(8,128)S(1)} copy-done((f32[16,8,128]{2,1,0:T(8,128)S(1)}, f32[16,8,128]{2,1,0:T(8,128)}, u32[]{:S(2)}) %copy-start.2) | copy-done | bytes 65560
  10.0 0.0 copy-start.3
  10.0 0.1 shard_map.41
  10.1 6.0 %collective-permute-start.1 = (f32[4,16,8,128]{3,2,1,0:T(8,128)S(1)}, f32[4,16,8,128]{3,2,1,0:T(8,128)S(1)}, u32[]{:S(2)}, u32[]{:S(2)}) collective-permute-start(f32[4,16,8,128]{3,2,1,0:T(8,128)S(1)} %get-tuple-element.14), channel_id=1, source_target_pairs={{1,0},{0,1},{3,2},{5,4},{7,6},{6,7},{8,9},{11,10},{10,11},{13,12},... | collective-permute-start | bytes 786440 | tf_op jit(solution)/shard_map/ppermute | solution.py:554
  16.1 1.9 %collective-permute-start.2 = (f32[4,16,8,128]{3,2,1,0:T(8,128)S(1)}, f32[4,16,8,128]{3,2,1,0:T(8,128)S(1)}, u32[]{:S(2)}, u32[]{:S(2)}) collective-permute-start(f32[4,16,8,128]{3,2,1,0:T(8,128)S(1)} %get-tuple-element.15), channel_id=1, source_target_pairs={{4,0},{5,1},{6,2},{0,4},{2,6},{3,7},{13,9},{14,10},{15,11},{8,12},... | collective-permute-start | bytes 786440 | tf_op jit(solution)/shard_map/ppermute | solution.py:554
  18.0 1.3 %collective-permute-start.3 = (f32[4,16,8,128]{3,2,1,0:T(8,128)S(1)}, f32[4,16,8,128]{3,2,1,0:T(8,128)S(1)}, u32[]{:S(2)}, u32[]{:S(2)}) collective-permute-start(f32[4,16,8,128]{3,2,1,0:T(8,128)S(1)} %get-tuple-element.16), channel_id=1, source_target_pairs={{5,0},{4,1},{7,2},{1,4},{3,6},{2,7},{12,9},{15,10},{14,11},{9,12},... | collective-permute-start | bytes 786440 | tf_op jit(solution)/shard_map/ppermute | solution.py:554
  19.3 0.0 collective-permute-done.4.refs_6_
  19.3 4.1 %collective-permute-start.6 = (f32[2,16,8,128]{3,2,1,0:T(8,128)S(1)}, f32[2,16,8,128]{3,2,1,0:T(8,128)S(1)}, u32[]{:S(2)}, u32[]{:S(2)}) collective-permute-start(f32[2,16,8,128]{3,2,1,0:T(8,128)S(1)} %get-tuple-element.19), channel_id=1, source_target_pairs={{6,0},{7,1},{4,2},{2,4},{0,6},{1,7},{15,9},{12,10},{13,11},{10,12}... | collective-permute-start | bytes 393224 | tf_op jit(solution)/shard_map/ppermute | solution.py:554
  23.4 0.0 collective-permute-done.5.refs_7_
  23.4 7.1 %collective-permute-start.7 = (f32[2,16,8,128]{3,2,1,0:T(8,128)S(1)}, f32[2,16,8,128]{3,2,1,0:T(8,128)S(1)}, u32[]{:S(2)}, u32[]{:S(2)}) collective-permute-start(f32[2,16,8,128]{3,2,1,0:T(8,128)S(1)} %get-tuple-element.20), channel_id=1, source_target_pairs={{7,0},{6,1},{5,2},{3,4},{1,6},{0,7},{14,9},{13,10},{12,11},{11,12}... | collective-permute-start | bytes 393224 | tf_op jit(solution)/shard_map/ppermute | solution.py:554
  30.5 0.0 collective-permute-done.6.refs_8_
  30.5 4.2 %collective-permute-done.7.refs_9_ = f32[2,16,8,128]{3,2,1,0:T(8,128)S(1)} collective-permute-done((f32[2,16,8,128]{3,2,1,0:T(8,128)S(1)}, f32[2,16,8,128]{3,2,1,0:T(8,128)S(1)}, u32[]{:S(2)}, u32[]{:S(2)}) %collective-permute-start.7) | collective-permute-done | bytes 131104 | tf_op jit(solution)/shard_map/ppermute | solution.py:554
  34.7 0.0 collective-permute-done.1.refs_3_
  34.7 1.2 %collective-permute-done.2.refs_4_ = f32[4,16,8,128]{3,2,1,0:T(8,128)S(1)} collective-permute-done((f32[4,16,8,128]{3,2,1,0:T(8,128)S(1)}, f32[4,16,8,128]{3,2,1,0:T(8,128)S(1)}, u32[]{:S(2)}, u32[]{:S(2)}) %collective-permute-start.2) | collective-permute-done | bytes 262176 | tf_op jit(solution)/shard_map/ppermute | solution.py:554
  35.9 0.0 collective-permute-done.3.refs_5_
  35.9 0.0 copy-done.1
  35.9 0.0 copy-done.3
  35.9 13.0 %shard_map.43 = (f32[4,16,8,128]{3,2,1,0:T(8,128)S(1)}, f32[4,16,8,128]{3,2,1,0:T(8,128)S(1)}, f32[4,16,8,128]{3,2,1,0:T(8,128)S(1)}, f32[4,16,8,128]{3,2,1,0:T(8,128)S(1)}, f32[4,16,8,128]{3,2,1,0:T(8,128)S(1)}) custom-call(f32[2,3,16,8,128]{4,3,2,1,0:T(8,128)S(1)} %copy-done.1, f32[16,8,128]{2,1,0:T(8,128)S(1)} %copy-done.3, ...), custom_call_target="tpu_custom_call" | custom-call | tf_op jit(solution)/shard_map/pallas_call | solution.py:530
  49.0 4.5 %collective-permute-start.8 = (f32[4,16,8,128]{3,2,1,0:T(8,128)S(1)}, f32[4,16,8,128]{3,2,1,0:T(8,128)S(1)}, u32[]{:S(2)}, u32[]{:S(2)}) collective-permute-start(f32[4,16,8,128]{3,2,1,0:T(8,128)S(1)} %get-tuple-element.22), channel_id=1, source_target_pairs={{1,0},{0,1},{2,3},{4,5},{7,6},{6,7},{9,8},{11,10},{10,11},{13,12},... | collective-permute-start | bytes 786440 | tf_op jit(solution)/shard_map/ppermute | solution.py:584
  53.5 0.7 %collective-permute-start.9 = (f32[4,16,8,128]{3,2,1,0:T(8,128)S(1)}, f32[4,16,8,128]{3,2,1,0:T(8,128)S(1)}, u32[]{:S(2)}, u32[]{:S(2)}) collective-permute-start(f32[4,16,8,128]{3,2,1,0:T(8,128)S(1)} %get-tuple-element.23), channel_id=1, source_target_pairs={{6,3},{1,4},{2,7},{13,8},{9,12},{10,15},{22,19},{17,20},{18,23},{2... | collective-permute-start | bytes 786440 | tf_op jit(solution)/shard_map/ppermute | solution.py:584
  54.2 1.9 %collective-permute-start.10 = (f32[4,16,8,128]{3,2,1,0:T(8,128)S(1)}, f32[4,16,8,128]{3,2,1,0:T(8,128)S(1)}, u32[]{:S(2)}, u32[]{:S(2)}) collective-permute-start(f32[4,16,8,128]{3,2,1,0:T(8,128)S(1)} %get-tuple-element.24), channel_id=1, source_target_pairs={{4,0},{6,2},{7,3},{0,4},{1,5},{2,6},{12,8},{13,9},{15,11},{9,13},{... | collective-permute-start | bytes 786440 | tf_op jit(solution)/shard_map/ppermute | solution.py:584
  56.1 0.7 %collective-permute-start.11 = (f32[4,16,8,128]{3,2,1,0:T(8,128)S(1)}, f32[4,16,8,128]{3,2,1,0:T(8,128)S(1)}, u32[]{:S(2)}, u32[]{:S(2)}) collective-permute-start(f32[4,16,8,128]{3,2,1,0:T(8,128)S(1)} %get-tuple-element.25), channel_id=1, source_target_pairs={{2,1},{1,2},{6,5},{10,9},{9,10},{13,14},{18,17},{17,18},{22,21},{2... | collective-permute-start | bytes 786440 | tf_op jit(solution)/shard_map/ppermute | solution.py:584
  56.8 3.8 %collective-permute-done.8.refs_1_ = f32[4,16,8,128]{3,2,1,0:T(8,128)S(1)} collective-permute-done((f32[4,16,8,128]{3,2,1,0:T(8,128)S(1)}, f32[4,16,8,128]{3,2,1,0:T(8,128)S(1)}, u32[]{:S(2)}, u32[]{:S(2)}) %collective-permute-start.8) | collective-permute-done | bytes 262176 | tf_op jit(solution)/shard_map/ppermute | solution.py:584
  60.6 0.0 collective-permute-done.9.refs_2_
  60.6 5.0 %collective-permute-done.10.refs_3_ = f32[4,16,8,128]{3,2,1,0:T(8,128)S(1)} collective-permute-done((f32[4,16,8,128]{3,2,1,0:T(8,128)S(1)}, f32[4,16,8,128]{3,2,1,0:T(8,128)S(1)}, u32[]{:S(2)}, u32[]{:S(2)}) %collective-permute-start.10) | collective-permute-done | bytes 262176 | tf_op jit(solution)/shard_map/ppermute | solution.py:584
  65.6 0.0 collective-permute-done.11.refs_4_
  65.6 0.9 %shard_map.44 = (f32[2,3,16,8,128]{4,3,2,1,0:T(8,128)}, f32[2,3,16,8,128]{4,3,2,1,0:T(8,128)}) custom-call(f32[4,16,8,128]{3,2,1,0:T(8,128)S(1)} %get-tuple-element.21.refs_0_, f32[4,16,8,128]{3,2,1,0:T(8,128)S(1)} %collective-permute-done.8.refs_1_, f32[4,16,8,128]{3,2,1,0:T(8,128)S(1)} %collective-permute-done.9.refs_2_, ...), custom_call_target="tpu_custom_call" | custom-call | tf_op jit(solution)/shard_map/pallas_call | solution.py:530
  (1 shorter events, 0.0 us)
Async XLA Ops:
  0.6 8.5 %collective-permute-start = (f32[16,8,128]{2,1,0:T(8,128)}, f32[16,8,128]{2,1,0:T(8,128)S(1)}, u32[]{:S(2)}, u32[]{:S(2)}) collective-permute-start(f32[16,8,128]{2,1,0:T(8,128)} %refs_1_.1), channel_id=1, source_target_pairs={{2,0},{3,1},{0,2},{1,3},{6,4},{7,5},{4,6},{5,7},{10,8},{11,9},{8,1... | collective-permute-start | bytes 196616 | tf_op jit(solution)/shard_map/ppermute | solution.py:554
  4.8 1.0 %copy-start = (f32[2,3,16,8,128]{4,3,2,1,0:T(8,128)S(1)}, f32[2,3,16,8,128]{4,3,2,1,0:T(8,128)}, u32[]{:S(2)}) copy-start(f32[2,3,16,8,128]{4,3,2,1,0:T(8,128)} %refs_0_.1) | copy-start | bytes 1179652
  5.8 30.2 %copy-start.1 = (f32[2,3,16,8,128]{4,3,2,1,0:T(8,128)S(1)}, f32[2,3,16,8,128]{4,3,2,1,0:T(8,128)}, u32[]{:S(2)}) copy-start(f32[2,3,16,8,128]{4,3,2,1,0:T(8,128)} %refs_0_.1) | copy-start | bytes 1179652
  5.8 13.5 %collective-permute-start.4 = (f32[2,16,8,128]{3,2,1,0:T(8,128)S(1)}, f32[2,16,8,128]{3,2,1,0:T(8,128)S(1)}, u32[]{:S(2)}, u32[]{:S(2)}) collective-permute-start(f32[2,16,8,128]{3,2,1,0:T(8,128)S(1)} %get-tuple-element.17), channel_id=1, source_target_pairs={{2,0},{3,1},{0,2},{6,4},{4,6},{5,7},{11,9},{8,10},{9,11},{14,12},{... | collective-permute-start | bytes 393224 | tf_op jit(solution)/shard_map/ppermute | solution.py:554
  7.9 15.6 %collective-permute-start.5 = (f32[2,16,8,128]{3,2,1,0:T(8,128)S(1)}, f32[2,16,8,128]{3,2,1,0:T(8,128)S(1)}, u32[]{:S(2)}, u32[]{:S(2)}) collective-permute-start(f32[2,16,8,128]{3,2,1,0:T(8,128)S(1)} %get-tuple-element.18), channel_id=1, source_target_pairs={{3,0},{2,1},{1,2},{7,4},{5,6},{4,7},{10,9},{9,10},{8,11},{15,12},{... | collective-permute-start | bytes 393224 | tf_op jit(solution)/shard_map/ppermute | solution.py:554
  9.2 0.8 %copy-start.2 = (f32[16,8,128]{2,1,0:T(8,128)S(1)}, f32[16,8,128]{2,1,0:T(8,128)}, u32[]{:S(2)}) copy-start(f32[16,8,128]{2,1,0:T(8,128)} %refs_1_.1) | copy-start | bytes 196612
  10.0 25.9 %copy-start.3 = (f32[16,8,128]{2,1,0:T(8,128)S(1)}, f32[16,8,128]{2,1,0:T(8,128)}, u32[]{:S(2)}) copy-start(f32[16,8,128]{2,1,0:T(8,128)} %refs_1_.1) | copy-start | bytes 196612
  10.1 24.6 %collective-permute-start.1 = (f32[4,16,8,128]{3,2,1,0:T(8,128)S(1)}, f32[4,16,8,128]{3,2,1,0:T(8,128)S(1)}, u32[]{:S(2)}, u32[]{:S(2)}) collective-permute-start(f32[4,16,8,128]{3,2,1,0:T(8,128)S(1)} %get-tuple-element.14), channel_id=1, source_target_pairs={{1,0},{0,1},{3,2},{5,4},{7,6},{6,7},{8,9},{11,10},{10,11},{13,12},... | collective-permute-start | bytes 786440 | tf_op jit(solution)/shard_map/ppermute | solution.py:554
  16.1 19.8 %collective-permute-start.2 = (f32[4,16,8,128]{3,2,1,0:T(8,128)S(1)}, f32[4,16,8,128]{3,2,1,0:T(8,128)S(1)}, u32[]{:S(2)}, u32[]{:S(2)}) collective-permute-start(f32[4,16,8,128]{3,2,1,0:T(8,128)S(1)} %get-tuple-element.15), channel_id=1, source_target_pairs={{4,0},{5,1},{6,2},{0,4},{2,6},{3,7},{13,9},{14,10},{15,11},{8,12},... | collective-permute-start | bytes 786440 | tf_op jit(solution)/shard_map/ppermute | solution.py:554
  18.0 17.9 %collective-permute-start.3 = (f32[4,16,8,128]{3,2,1,0:T(8,128)S(1)}, f32[4,16,8,128]{3,2,1,0:T(8,128)S(1)}, u32[]{:S(2)}, u32[]{:S(2)}) collective-permute-start(f32[4,16,8,128]{3,2,1,0:T(8,128)S(1)} %get-tuple-element.16), channel_id=1, source_target_pairs={{5,0},{4,1},{7,2},{1,4},{3,6},{2,7},{12,9},{15,10},{14,11},{9,12},... | collective-permute-start | bytes 786440 | tf_op jit(solution)/shard_map/ppermute | solution.py:554
  19.3 11.2 %collective-permute-start.6 = (f32[2,16,8,128]{3,2,1,0:T(8,128)S(1)}, f32[2,16,8,128]{3,2,1,0:T(8,128)S(1)}, u32[]{:S(2)}, u32[]{:S(2)}) collective-permute-start(f32[2,16,8,128]{3,2,1,0:T(8,128)S(1)} %get-tuple-element.19), channel_id=1, source_target_pairs={{6,0},{7,1},{4,2},{2,4},{0,6},{1,7},{15,9},{12,10},{13,11},{10,12}... | collective-permute-start | bytes 393224 | tf_op jit(solution)/shard_map/ppermute | solution.py:554
  23.4 11.3 %collective-permute-start.7 = (f32[2,16,8,128]{3,2,1,0:T(8,128)S(1)}, f32[2,16,8,128]{3,2,1,0:T(8,128)S(1)}, u32[]{:S(2)}, u32[]{:S(2)}) collective-permute-start(f32[2,16,8,128]{3,2,1,0:T(8,128)S(1)} %get-tuple-element.20), channel_id=1, source_target_pairs={{7,0},{6,1},{5,2},{3,4},{1,6},{0,7},{14,9},{13,10},{12,11},{11,12}... | collective-permute-start | bytes 393224 | tf_op jit(solution)/shard_map/ppermute | solution.py:554
  49.0 11.7 %collective-permute-start.8 = (f32[4,16,8,128]{3,2,1,0:T(8,128)S(1)}, f32[4,16,8,128]{3,2,1,0:T(8,128)S(1)}, u32[]{:S(2)}, u32[]{:S(2)}) collective-permute-start(f32[4,16,8,128]{3,2,1,0:T(8,128)S(1)} %get-tuple-element.22), channel_id=1, source_target_pairs={{1,0},{0,1},{2,3},{4,5},{7,6},{6,7},{9,8},{11,10},{10,11},{13,12},... | collective-permute-start | bytes 786440 | tf_op jit(solution)/shard_map/ppermute | solution.py:584
  53.5 7.1 %collective-permute-start.9 = (f32[4,16,8,128]{3,2,1,0:T(8,128)S(1)}, f32[4,16,8,128]{3,2,1,0:T(8,128)S(1)}, u32[]{:S(2)}, u32[]{:S(2)}) collective-permute-start(f32[4,16,8,128]{3,2,1,0:T(8,128)S(1)} %get-tuple-element.23), channel_id=1, source_target_pairs={{6,3},{1,4},{2,7},{13,8},{9,12},{10,15},{22,19},{17,20},{18,23},{2... | collective-permute-start | bytes 786440 | tf_op jit(solution)/shard_map/ppermute | solution.py:584
  54.2 11.4 %collective-permute-start.10 = (f32[4,16,8,128]{3,2,1,0:T(8,128)S(1)}, f32[4,16,8,128]{3,2,1,0:T(8,128)S(1)}, u32[]{:S(2)}, u32[]{:S(2)}) collective-permute-start(f32[4,16,8,128]{3,2,1,0:T(8,128)S(1)} %get-tuple-element.24), channel_id=1, source_target_pairs={{4,0},{6,2},{7,3},{0,4},{1,5},{2,6},{12,8},{13,9},{15,11},{9,13},{... | collective-permute-start | bytes 786440 | tf_op jit(solution)/shard_map/ppermute | solution.py:584
  56.1 9.5 %collective-permute-start.11 = (f32[4,16,8,128]{3,2,1,0:T(8,128)S(1)}, f32[4,16,8,128]{3,2,1,0:T(8,128)S(1)}, u32[]{:S(2)}, u32[]{:S(2)}) collective-permute-start(f32[4,16,8,128]{3,2,1,0:T(8,128)S(1)} %get-tuple-element.25), channel_id=1, source_target_pairs={{2,1},{1,2},{6,5},{10,9},{9,10},{13,14},{18,17},{17,18},{22,21},{2... | collective-permute-start | bytes 786440 | tf_op jit(solution)/shard_map/ppermute | solution.py:584
